TPU v7x, 32 devices: a whole 2x2x4 slice. The times are simulated.
32 devices in a mesh: parts: 2 (over x), genes: 8 (over z, y), samples: 2 (over core).
Axes of the slice: x: 2, y: 2, z: 4, core: 2. Of those that a mesh axis runs over, the one named last changes fastest.
Arguments:
- dosage: bfloat16 [32768, 2048], P(('parts', 'genes'), 'samples'), parts along dimension 0, may hold values from -6 to 6
- expression: bfloat16 [128, 2048], P(('parts', 'genes'), 'samples'), parts along dimension 0, may hold values from -6 to 6
- intron_counts: bfloat16 [4096, 2560], P(('parts', 'samples', 'genes')), parts along dimension 0, may hold values from 1 to 100
- cluster_sizes: int32 [128, 8], P('parts'), parts along dimension 0, may hold values from 1 to 12, 40 in all within a row
- valid_mask: int32 [128, 40], P('parts'), parts along dimension 0, may hold values 0 or 1
- gene_block: int32 [128], P('parts'), parts along dimension 0, may hold values from 0 to 63, each once
- window_start: int32 [128], P(('parts', 'genes')), parts along dimension 0, may hold values from 0 to 1024, as said below
Outputs:
- assoc: bfloat16 [128, 41, 2048], P(('parts', 'genes'), None, 'samples'), parts along dimension 0
There are 2 independent parts, one for each index of `parts`. A program takes and returns all parts, laid end to end along the dimension named above; each array names one. Nothing has to cross between parts.
Inputs may be any that keep to these rules, and one draw needn't show every extreme that they name: Every window_start is a multiple of 128 and at most 1024; some gene reaches 1024 in every draw. `gene_block`: a permutation of the genes. `cluster_sizes`: each row sums to 40.
All inputs are finite; a program needn't handle non-finite values.
Results may differ from a plain program's by a relative error of at most 0.0058.
Values may be sent and summed in bfloat16 or wider, within the bound.
A program may use at most 64 MiB of HBM per device.

v0:
```python
import jax
import jax.numpy as jnp
from jax import lax
from jax.sharding import PartitionSpec as P

W = 2048
SLOTS = 40
SPILL = 1024
ALIGN = 128


def shifted(block, axis, distance):
    devices = range(lax.axis_size(axis))
    route = [(i - distance, i) for i in devices if i - distance in devices]
    return lax.ppermute(block, axis, route)


def cluster_ratios(counts, cluster_sizes, valid_mask):
    cluster_ends = jnp.cumsum(cluster_sizes, axis=1, dtype=jnp.int32)
    slot_index = jnp.arange(SLOTS, dtype=jnp.int32)
    cluster_id = jnp.sum(
        (cluster_ends[:, None, :] <= slot_index[None, :, None]).astype(jnp.int32),
        axis=2,
        dtype=jnp.int32,
    )
    same_cluster = (cluster_id[:, :, None] == cluster_id[:, None, :]).astype(jnp.float32)
    live_counts = counts * valid_mask.astype(jnp.float32)[None, :, :]
    cluster_total = jnp.einsum(
        "sgj,gjk->sgk", live_counts, same_cluster, precision=lax.Precision.HIGHEST
    )
    return (live_counts / jnp.maximum(cluster_total, 1.0)).astype(jnp.bfloat16)


def tile_window(owner_block, offset, width):
    leading = owner_block.shape[:-1]
    tiles = owner_block.reshape(leading + (owner_block.shape[-1] // ALIGN, ALIGN))
    first_tile = offset // ALIGN
    piece = lax.dynamic_slice_in_dim(tiles, first_tile, width // ALIGN, len(leading))
    return piece.reshape(leading + (width,))


def window_slices(product, row_sum, row_square, starts, width):

    def window_of(owner_block, offset):
        return tile_window(owner_block, offset, width)

    cross_part = jax.vmap(window_of, in_axes=(0, 0))(product, starts)
    sum_part = jax.vmap(window_of, in_axes=(None, 0))(row_sum, starts)
    square_part = jax.vmap(window_of, in_axes=(None, 0))(row_square, starts)
    return (cross_part, sum_part, square_part)


def finish_stats(cross_part, sum_part, square_part, phen_sum, phen_square, sample_count):
    numerator = cross_part - sum_part[:, None, :] * phen_sum[:, :, None] / sample_count
    dose_var = jnp.maximum(square_part - sum_part * sum_part / sample_count, 1.0)
    pheno_var = jnp.maximum(phen_square - phen_sum * phen_sum / sample_count, 1.0)
    return (numerator * lax.rsqrt(dose_var)[:, None, :] * lax.rsqrt(pheno_var)[:, :, None]).astype(
        jnp.bfloat16
    )


def shards(dosage, expression, intron_counts, cluster_sizes, valid_mask, gene_block, window_start):
    samp_dev = dosage.shape[1]
    gene_dev = expression.shape[0]
    total_genes = gene_block.shape[0]
    next_rows = shifted(dosage[:SPILL], "genes", -1)
    dose_rows = jnp.concatenate([dosage, next_rows], axis=0)
    stored = intron_counts.reshape(intron_counts.shape[0], total_genes, SLOTS)
    counts = jnp.take(stored, gene_block, axis=1).astype(jnp.float32)
    ratios = cluster_ratios(counts, cluster_sizes, valid_mask).reshape(
        intron_counts.shape[0], total_genes * SLOTS
    )
    exchanged = lax.all_to_all(ratios, "genes", split_axis=1, concat_axis=0, tiled=True)
    intron_panel = exchanged.reshape(samp_dev, gene_dev, SLOTS)
    n_samples = lax.axis_size("samples")
    half_width = W // n_samples
    offset = lax.axis_index("samples") * half_width
    contract = (((0,), (1,)), ((), ()))
    expr_product = lax.dot_general(
        expression, dose_rows, (((1,), (1,)), ((), ())), preferred_element_type=jnp.float32
    )
    intron_product = lax.dot_general(
        exchanged, dose_rows, contract, preferred_element_type=jnp.float32
    )
    intron_product = intron_product.reshape(gene_dev, SLOTS, W + SPILL)
    product = jnp.concatenate([expr_product[:, None, :], intron_product], axis=1)
    expr_float = expression.astype(jnp.float32)
    intron_float = intron_panel.astype(jnp.float32)
    phen_sum = jnp.concatenate(
        [jnp.sum(expr_float, axis=1)[:, None], jnp.sum(intron_float, axis=0)], axis=1
    )
    phen_square = jnp.concatenate(
        [
            jnp.sum(expr_float * expr_float, axis=1)[:, None],
            jnp.sum(intron_float * intron_float, axis=0),
        ],
        axis=1,
    )
    dose_float = dose_rows.astype(jnp.float32)
    row_sum = jnp.sum(dose_float, axis=1)
    row_square = jnp.sum(dose_float * dose_float, axis=1)
    row_sum, row_square, phen_sum, phen_square = lax.psum(
        (row_sum, row_square, phen_sum, phen_square), "samples"
    )
    cross_part, sum_part, square_part = window_slices(product, row_sum, row_square, window_start, W)
    cross_sums = lax.psum_scatter(cross_part, "samples", scatter_dimension=2, tiled=True)
    sum_half = lax.dynamic_slice_in_dim(sum_part, offset, half_width, 1)
    square_half = lax.dynamic_slice_in_dim(square_part, offset, half_width, 1)
    sample_count = float(samp_dev * n_samples)
    return finish_stats(cross_sums, sum_half, square_half, phen_sum, phen_square, sample_count)


def solution(mesh):
    in_specs = (
        P(("parts", "genes"), "samples"),
        P(("parts", "genes"), "samples"),
        P(("parts", "samples", "genes"), None),
        P("parts", None),
        P("parts", None),
        P("parts"),
        P(("parts", "genes")),
    )
    out_specs = P(("parts", "genes"), None, "samples")
    return jax.shard_map(shards, mesh=mesh, in_specs=in_specs, out_specs=out_specs, check_vma=False)
```

profile of v0, /device:TPU:0, one launch (start us, length us, event | category | flops | bytes accessed | tf_op | source)
XLA Modules:
  0.0 140.2 jit_solution(9824551427102057853)
XLA Ops:
  6.5 3.2 %slice.3 = bf16[1024,1024]{1,0:T(8,128)(2,1)} slice(bf16[2048,1024]{1,0:T(8,128)(2,1)} %param.7), slice={[0:1024], [0:1024]} | slice | bytes 4194304 | tf_op jit(solution)/shard_map/slice | solution.py:66
  9.7 1.3 collective-permute-start
  11.1 0.3 copy.34
  11.5 0.1 copy.36
  11.7 0.7 gather_fusion
  12.4 3.1 %fusion.3 = bf16[128,64,40]{0,2,1:T(8,128)(2,1)} fusion(f32[64,40]{1,0:T(8,128)S(1)} %copy.35, bf16[64,128,40]{1,2,0:T(8,128)(2,1)S(1)} %gather_fusion, s32[64,40]{1,0:T(8,128)S(1)} %copy.36, pred[64]{0:T(512)(128)(4,1)S(1)} %compare_and_fusion), kind=kOutput, calls=%fused_computation.15 | convolution fusion | flops 160337920 | bytes 1331264 | tf_op jit(solution)/shard_map/sgj,gjk->sgk/dot_general | solution.py:28
  15.5 8.6 %all-to-all-start = ((bf16[128,8,320]{0,2,1:T(8,128)(2,1)}), bf16[128,8,320]{0,2,1:T(8,128)(2,1)S(1)}, u32[]{:S(2)}, u32[]{:S(2)}) async-start(bf16[128,8,320]{0,2,1:T(8,128)(2,1)} %bitcast.5), calls=%async_computation | async-start | bytes 1310720 | tf_op jit(solution)/shard_map/all_to_all | solution.py:73
  24.1 4.6 %constant_dynamic-update-slice_fusion.1 = bf16[3072,1024]{1,0:T(8,128)(2,1)} fusion(bf16[2048,1024]{1,0:T(8,128)(2,1)} %param.7), kind=kLoop, calls=%fused_computation.40 | loop fusion | bytes 8388608
  28.7 49.8 %all-to-all-done = bf16[128,8,320]{0,2,1:T(8,128)(2,1)S(1)} async-done(((bf16[128,8,320]{0,2,1:T(8,128)(2,1)}), bf16[128,8,320]{0,2,1:T(8,128)(2,1)S(1)}, u32[]{:S(2)}, u32[]{:S(2)}) %all-to-all-start) | async-done | bytes 655392 | tf_op jit(solution)/shard_map/all_to_all | solution.py:73
  78.5 0.1 copy_bitcast_fusion
  78.6 1.5 %constant_dynamic-update-slice_fusion = bf16[3072,1024]{1,0:T(8,128)(2,1)} fusion(bf16[3072,1024]{1,0:T(8,128)(2,1)} %constant_dynamic-update-slice_fusion.1, bf16[1024,1024]{1,0:T(8,128)(2,1)S(1)} %collective-permute-done), kind=kLoop, calls=%fused_computation.39 | loop fusion | bytes 4194304 | tf_op jit(solution)/shard_map/concatenate | solution.py:67
  80.1 4.7 %convolution_bitcast_fusion = f32[8,1,24,128]{3,0,2,1:T(8,128)S(1)} fusion(bf16[3072,1024]{1,0:T(8,128)(2,1)} %constant_dynamic-update-slice_fusion, bf16[8,1024]{1,0:T(8,128)(2,1)S(1)} %copy-done.4), kind=kOutput, calls=%fused_computation.22 | convolution fusion | flops 50331648 | bytes 6406144 | tf_op jit(solution)/shard_map/dot_general | solution.py:79
  84.7 0.1 copy.39
  84.9 2.3 %fusion.18 = f32[8,40,24,128]{3,1,2,0:T(8,128)S(1)} fusion(bf16[8,40,1024,1]{2,1,3,0:T(8,128)(2,1)S(1)} %bitcast.75, bf16[24,128,1024,1]{2,1,0,3:T(8,128)(2,1)S(1)} %bitcast.73), kind=kOutput, calls=%fused_computation.55 | convolution fusion | flops 2013265920 | bytes 10878976 | tf_op jit(solution)/shard_map/dot_general | solution.py:82
  87.2 0.5 pad_maximum_fusion
  87.7 2.7 %copy.40 = f32[8,41,24,128]{3,1,0,2:T(8,128)} copy(f32[8,41,24,128]{3,1,2,0:T(8,128)S(1)} %pad_maximum_fusion) | data formatting | bytes 8060928 | tf_op jit(solution)/shard_map/concatenate | solution.py:86
  90.4 3.1 %gather_fusion.1 = f32[8,41,16,128]{3,1,2,0:T(8,128)S(1)} fusion(f32[8,41,24,128]{3,1,0,2:T(8,128)} %copy.40, s32[8]{0:T(128)S(1)} %or_bitcast_fusion), kind=kCustom, calls=%fused_computation.1 | custom fusion | bytes 5374080 | tf_op jit(solution)/shard_map/vmap()/gather | solution.py:38
  93.5 2.4 %copy.41 = f32[8,41,16,128]{3,2,0,1:T(8,128)} copy(f32[8,41,16,128]{3,1,2,0:T(8,128)S(1)} %gather_fusion.1) | data formatting | bytes 5373952 | tf_op jit(solution)/shard_map/vmap()/gather | solution.py:38
  95.9 3.9 %reshape.50 = f32[8,41,2048]{2,0,1:T(8,128)} reshape(f32[8,41,16,128]{3,2,0,1:T(8,128)} %copy.41) | data formatting | bytes 5373952 | tf_op jit(solution)/shard_map/vmap()/reshape | solution.py:39
  99.8 0.1 convert_reduce_fusion.3
  100.0 0.1 copy.42
  100.0 0.1 copy.44
  100.2 0.7 copy-done.2
  100.9 0.3 convert_reduce_fusion.1
  101.3 0.1 pad_maximum_fusion.1
  101.4 5.5 %convert_reduce_fusion = (f32[3072]{0:T(1024)S(1)}, f32[3072]{0:T(1024)S(1)}) fusion(bf16[3072,1024]{1,0:T(8,128)(2,1)} %constant_dynamic-update-slice_fusion), kind=kLoop, calls=%fused_computation.7 | loop fusion | flops 12576768 | bytes 6316032 | tf_op jit(solution)/shard_map/reduce_sum | solution.py:100
  106.9 3.4 %all-reduce.1 = (f32[8,41]{1,0:T(8,128)S(1)}, f32[8,41]{1,0:T(8,128)S(1)}, f32[24,128]{1,0:T(8,128)S(1)}, f32[24,128]{1,0:T(8,128)S(1)}) all-reduce(f32[8,41]{1,0:T(8,128)S(1)} %get-tuple-element.50, f32[8,41]{1,0:T(8,128)S(1)} %get-tuple-element.49, ...), channel_id=1, replica_groups=mesh['parts'=2,'genes'=8,'samples'=2] {'samples'}, use_global_device_ids=true, to_apply=%region_12.13 | all-reduce | flops 6800 | bytes 54400 | tf_op jit(solution)/shard_map/psum | solution.py:102
  110.3 10.1 %while.3 = (s32[]{:T(128)}, f32[24,128]{1,0:T(8,128)S(1)}, s32[8,2]{0,1:T(2,128)S(1)}, f32[8,16,128]{2,1,0:T(8,128)S(1)}, s32[]{:T(128)}) while((s32[]{:T(128)}, f32[24,128]{1,0:T(8,128)S(1)}, s32[8,2]{0,1:T(2,128)S(1)}, f32[8,16,128]{2,1,0:T(8,128)S(1)}, s32[]{:T(128)}) %tuple.35), condition=%wide.while_cond.1, body=%wide.while_body.1.sunk | while | flops 2 | bytes 16481 | solution.py:38
  110.4 0.5 slice.35
  110.9 0.7 bitcast_dynamic-update-slice_fusion.5
  111.7 0.5 slice.35
  112.2 0.7 bitcast_dynamic-update-slice_fusion.5
  112.9 0.5 slice.35
  113.4 0.7 bitcast_dynamic-update-slice_fusion.5
  114.2 0.5 slice.35
  114.7 0.7 bitcast_dynamic-update-slice_fusion.5
  115.5 0.5 slice.35
  116.0 0.7 bitcast_dynamic-update-slice_fusion.5
  116.7 0.5 slice.35
  117.2 0.7 bitcast_dynamic-update-slice_fusion.5
  118.0 0.5 slice.35
  118.5 0.7 bitcast_dynamic-update-slice_fusion.5
  119.3 0.5 slice.35
  119.8 0.7 bitcast_dynamic-update-slice_fusion.5
  120.5 10.1 %while.2 = (s32[]{:T(128)}, f32[24,128]{1,0:T(8,128)S(1)}, s32[8,2]{0,1:T(2,128)S(1)}, f32[8,16,128]{2,1,0:T(8,128)S(1)}, s32[]{:T(128)}) while((s32[]{:T(128)}, f32[24,128]{1,0:T(8,128)S(1)}, s32[8,2]{0,1:T(2,128)S(1)}, f32[8,16,128]{2,1,0:T(8,128)S(1)}, s32[]{:T(128)}) %tuple.40), condition=%wide.while_cond, body=%wide.while_body.sunk | while | flops 2 | bytes 16481 | solution.py:38
  120.6 0.5 slice.34
  121.1 0.7 bitcast_dynamic-update-slice_fusion.4
  121.8 0.5 slice.34
  122.4 0.7 bitcast_dynamic-update-slice_fusion.4
  123.1 0.5 slice.34
  123.6 0.7 bitcast_dynamic-update-slice_fusion.4
  124.4 0.5 slice.34
  124.9 0.7 bitcast_dynamic-update-slice_fusion.4
  125.6 0.5 slice.34
  126.1 0.7 bitcast_dynamic-update-slice_fusion.4
  126.9 0.5 slice.34
  127.4 0.7 bitcast_dynamic-update-slice_fusion.4
  128.2 0.5 slice.34
  128.7 0.7 bitcast_dynamic-update-slice_fusion.4
  129.4 0.5 slice.34
  129.9 0.7 bitcast_dynamic-update-slice_fusion.4
  130.6 0.1 copy.43
  130.7 0.1 copy.45
  130.9 2.5 %multiply_convert_fusion = bf16[8,41,1024]{2,0,1:T(8,128)(2,1)} fusion(f32[8,41,1024]{2,0,1:T(8,128)} %reduce-scatter.2.cloned.1.call-done, f32[8,41]{0,1:T(8,128)S(1)} %copy.45, f32[8,1024]{1,0:T(8,128)S(1)} %get-tuple-element.48, f32[8,41]{0,1:T(8,128)S(1)} %copy.43, f32[8,1024]{1,0:T(8,128)S(1)} %get-tuple-element.47), kind=kLoop, calls=%fused_computation.16 | loop fusion | flops 2015232 | bytes 2083392 | tf_op jit(solution)/shard_map/convert_element_type | solution.py:57
  (55 shorter events, 1.7 us)
Async XLA Ops:
  6.5 4.5 %copy-start.7 = (s32[64]{0:T(128)S(1)}, s32[64]{0:T(128)}, u32[]{:S(2)}) copy-start(s32[64]{0:T(128)} %param.12) | copy-start | bytes 772
  6.5 4.5 %copy-start.6 = (s32[64,8]{0,1:T(8,128)S(1)}, s32[64,8]{0,1:T(8,128)}, u32[]{:S(2)}) copy-start(s32[64,8]{0,1:T(8,128)} %param.10) | copy-start | bytes 6148
  6.5 4.6 %copy-start.3 = (bf16[128,2560]{1,0:T(8,128)(2,1)S(1)}, bf16[128,2560]{1,0:T(8,128)(2,1)}, u32[]{:S(2)}) copy-start(bf16[128,2560]{1,0:T(8,128)(2,1)} %param.9) | copy-start | bytes 1966084
  6.5 5.0 %copy-start.5 = (s32[64,40]{0,1:T(8,128)S(1)}, s32[64,40]{0,1:T(8,128)}, u32[]{:S(2)}) copy-start(s32[64,40]{0,1:T(8,128)} %param.11) | copy-start | bytes 30724
  9.7 68.9 %collective-permute-start = (bf16[1024,1024]{1,0:T(8,128)(2,1)}, bf16[1024,1024]{1,0:T(8,128)(2,1)S(1)}, u32[]{:S(2)}, u32[]{:S(2)}) collective-permute-start(bf16[1024,1024]{1,0:T(8,128)(2,1)} %slice.3), channel_id=1, source_target_pairs={{2,0},{4,2},{6,4},{8,6},{10,8},{12,10},{14,12},{3,1},{5,3},{7,5},{... | collective-permute-start | bytes 6291464 | tf_op jit(solution)/shard_map/ppermute | solution.py:15
  12.4 11.7 %copy-start.8 = (s32[8]{0:T(128)S(1)}, s32[8]{0:T(128)}, u32[]{:S(2)}) copy-start(s32[8]{0:T(128)} %param.13) | copy-start | bytes 100
  15.5 63.0 %all-to-all-start = ((bf16[128,8,320]{0,2,1:T(8,128)(2,1)}), bf16[128,8,320]{0,2,1:T(8,128)(2,1)S(1)}, u32[]{:S(2)}, u32[]{:S(2)}) async-start(bf16[128,8,320]{0,2,1:T(8,128)(2,1)} %bitcast.5), calls=%async_computation | async-start | bytes 1310720 | tf_op jit(solution)/shard_map/all_to_all | solution.py:73
  24.0 106.9 %reduce-scatter.2.cloned.1.call-start = ((), (), s32[]{:S(2)}) async-start(), calls=%async_computation.2 | async-start | bytes 4030464 | tf_op jit(solution)/shard_map/reduce_scatter | solution.py:106
  28.7 51.4 %copy-start.4 = (bf16[8,1024]{1,0:T(8,128)(2,1)S(1)}, bf16[8,1024]{1,0:T(8,128)(2,1)}, u32[]{:S(2)}) copy-start(bf16[8,1024]{1,0:T(8,128)(2,1)} %param.8) | copy-start | bytes 49156
  78.5 1.6 %copy-start.1 = (bf16[128,8,320]{0,2,1:T(8,128)(2,1)}, bf16[128,8,320]{0,2,1:T(8,128)(2,1)S(1)}, u32[]{:S(2)}) copy-start(bf16[128,8,320]{0,2,1:T(8,128)(2,1)S(1)} %all-to-all-done) | copy-start | bytes 1966084
  80.1 4.8 %copy-start = (bf16[3072,1024]{1,0:T(8,128)(2,1)S(1)}, bf16[3072,1024]{1,0:T(8,128)(2,1)}, u32[]{:S(2)}) copy-start(bf16[3072,1024]{1,0:T(8,128)(2,1)} %constant_dynamic-update-slice_fusion) | copy-start | bytes 18874372
  99.8 1.1 copy-start.2
Sparse Core Ops, SparseCore 0:
  99.9 7.5 reduce-scatter.1
where the time goes:
time: 141 us; the launch traced here: 140 us
  waiting for transfers between devices  49.9 us (35%)
  local copies, waits for them, and re-layouts  43.9 us (31%)
  between operations  13.7 us (10%)
  matrix products  10 us (7%)
  starting transfers between devices  9.88 us (7%)
  other arithmetic  9.15 us (6%)
  blocking collectives  3.42 us (2%)
    all_to_all x1, waiting for transfers between devices, shards(): lax.all_to_all(ratios, 'genes', split_axis=1, concat_axis=0, tiled=True)  49.8 us
    gather x48, local copies, waits for them, and re-layouts  19.9 us
    all_to_all x1, starting transfers between devices, shards(): lax.all_to_all(ratios, 'genes', split_axis=1, concat_axis=0, tiled=True)  8.56 us
    unnamed x24, local copies, waits for them, and re-layouts  5.68 us
    reduce_sum x1, other arithmetic, shards(): row_sum = jnp.sum(dose_float, axis=1)  5.48 us
    gather x2, local copies, waits for them, and re-layouts, tile_window(): lax.dynamic_slice_in_dim(tiles, first_tile, width // ALIGN, len(leading))  5.48 us
    dot_general x1, matrix products, shards(): lax.dot_general(expression, dose_rows, (((1,), (1,)), ((), ())), preferre...  4.66 us
    reshape x1, local copies, waits for them, and re-layouts, tile_window(): return piece.reshape(leading + (width,))  3.89 us
  transfers between devices with their start and end apart: 3, of which 1 were waited for; matrix products, arithmetic and copies ran while one was open for 25% of the time, Pallas kernels for 0%

commit v1 on v0

--- a/solution.py
+++ b/solution.py
@@ -70,7 +70,9 @@
     ratios = cluster_ratios(counts, cluster_sizes, valid_mask).reshape(
         intron_counts.shape[0], total_genes * SLOTS
     )
-    exchanged = lax.all_to_all(ratios, "genes", split_axis=1, concat_axis=0, tiled=True)
+    shards_2 = jnp.split(ratios, lax.axis_size("genes"), axis=1)
+    incoming = lax.all_to_all(jnp.stack(shards_2), "genes", 0, 0)
+    exchanged = jnp.concatenate(incoming, axis=0)
     intron_panel = exchanged.reshape(samp_dev, gene_dev, SLOTS)
     n_samples = lax.axis_size("samples")
     half_width = W // n_samples

time: 141 us -> 141 us (level)
  local copies, waits for them, and re-layouts: 43.9 us -> 49 us
  waiting for transfers between devices: 49.9 us -> 45.5 us
    unnamed x24 -> x31, local copies, waits for them, and re-layouts: 5.68 us -> 10.2 us
    all_to_all x1, waiting for transfers between devices: 49.8 us -> 45.4 us  [shards(): incoming = lax.all_to_all(jnp.stack(shards_2), 'genes', 0, 0)]
  transfers between devices with their start and end apart: 3 -> 3, of which waited for: 1 -> 1; matrix products, arithmetic and copies ran while one was open for 25% -> 28% of each run, Pallas kernels for 0% -> 0%
where the time goes in v1:
time: 141 us; the launch traced here: 140 us
  local copies, waits for them, and re-layouts  49 us (35%)
  waiting for transfers between devices  45.5 us (32%)
  between operations  13.7 us (10%)
  starting transfers between devices  9.88 us (7%)
  matrix products  9.27 us (7%)
  other arithmetic  9.15 us (6%)
  blocking collectives  3.42 us (2%)
    all_to_all x1, waiting for transfers between devices, shards(): incoming = lax.all_to_all(jnp.stack(shards_2), 'genes', 0, 0)  45.4 us
    gather x48, local copies, waits for them, and re-layouts  19.9 us
    unnamed x31, local copies, waits for them, and re-layouts  10.2 us
    all_to_all x1, starting transfers between devices, shards(): incoming = lax.all_to_all(jnp.stack(shards_2), 'genes', 0, 0)  8.56 us
    reduce_sum x1, other arithmetic, shards(): row_sum = jnp.sum(dose_float, axis=1)  5.48 us
    gather x2, local copies, waits for them, and re-layouts, tile_window(): lax.dynamic_slice_in_dim(tiles, first_tile, width // ALIGN, len(leading))  5.48 us
    dot_general x1, matrix products, shards(): lax.dot_general(expression, dose_rows, (((1,), (1,)), ((), ())), preferre...  4.66 us
    reshape x1, local copies, waits for them, and re-layouts, tile_window(): return piece.reshape(leading + (width,))  3.89 us
  transfers between devices with their start and end apart: 3, of which 1 were waited for; matrix products, arithmetic and copies ran while one was open for 28% of the time, Pallas kernels for 0%

profile of v1, /device:TPU:0, one launch (start us, length us, event | category | flops | bytes accessed | tf_op | source)
XLA Modules:
  0.0 140.2 jit_solution(14498258872075226060)
XLA Ops:
  6.5 3.2 %slice.3 = bf16[1024,1024]{1,0:T(8,128)(2,1)} slice(bf16[2048,1024]{1,0:T(8,128)(2,1)} %param.7), slice={[0:1024], [0:1024]} | slice | bytes 4194304 | tf_op jit(solution)/shard_map/slice | solution.py:66
  9.7 1.3 collective-permute-start
  11.0 0.3 copy.40
  11.7 0.7 gather_fusion
  12.4 2.3 %fusion.3 = bf16[128,64,40]{0,2,1:T(8,128)(2,1)S(1)} fusion(f32[64,40]{1,0:T(8,128)S(1)} %copy.41, bf16[64,128,40]{1,2,0:T(8,128)(2,1)S(1)} %gather_fusion, s32[64,40]{1,0:T(8,128)S(1)} %copy.42, pred[64]{0:T(512)(128)(4,1)S(1)} %compare_and_fusion), kind=kOutput, calls=%fused_computation.15 | convolution fusion | flops 160337920 | bytes 1331264 | tf_op jit(solution)/shard_map/sgj,gjk->sgk/dot_general | solution.py:28
  14.7 0.6 fusion.22
  15.4 0.6 fusion.21
  16.0 0.6 fusion.20
  16.7 0.6 fusion.19
  17.3 0.6 fusion.18
  17.9 0.6 fusion.17
  18.6 0.6 fusion.16
  19.2 0.6 fusion.15
  19.9 8.6 %all-to-all-start = ((bf16[8,128,320]{1,2,0:T(8,128)(2,1)}), bf16[8,128,320]{1,2,0:T(8,128)(2,1)S(1)}, u32[]{:S(2)}, u32[]{:S(2)}) async-start(bf16[8,128,320]{1,2,0:T(8,128)(2,1)} %fusion.15), calls=%async_computation | async-start | bytes 1310720 | tf_op jit(solution)/shard_map/all_to_all | solution.py:74
  28.5 4.6 %constant_dynamic-update-slice_fusion.1 = bf16[3072,1024]{1,0:T(8,128)(2,1)} fusion(bf16[2048,1024]{1,0:T(8,128)(2,1)} %param.7), kind=kLoop, calls=%fused_computation.55 | loop fusion | bytes 8388608
  33.1 45.4 %all-to-all-done = bf16[8,128,320]{1,2,0:T(8,128)(2,1)S(1)} async-done(((bf16[8,128,320]{1,2,0:T(8,128)(2,1)}), bf16[8,128,320]{1,2,0:T(8,128)(2,1)S(1)}, u32[]{:S(2)}, u32[]{:S(2)}) %all-to-all-start) | async-done | bytes 655392 | tf_op jit(solution)/shard_map/all_to_all | solution.py:74
  78.6 1.5 %constant_dynamic-update-slice_fusion = bf16[3072,1024]{1,0:T(8,128)(2,1)} fusion(bf16[3072,1024]{1,0:T(8,128)(2,1)} %constant_dynamic-update-slice_fusion.1, bf16[1024,1024]{1,0:T(8,128)(2,1)S(1)} %collective-permute-done), kind=kLoop, calls=%fused_computation.54 | loop fusion | bytes 4194304 | tf_op jit(solution)/shard_map/concatenate | solution.py:67
  80.1 4.7 %convolution_bitcast_fusion = f32[8,1,24,128]{3,0,2,1:T(8,128)S(1)} fusion(bf16[3072,1024]{1,0:T(8,128)(2,1)} %constant_dynamic-update-slice_fusion, bf16[8,1024]{1,0:T(8,128)(2,1)S(1)} %copy-done.4), kind=kOutput, calls=%fused_computation.22 | convolution fusion | flops 50331648 | bytes 6406144 | tf_op jit(solution)/shard_map/dot_general | solution.py:81
  84.9 2.3 %fusion.26 = f32[8,40,24,128]{3,1,2,0:T(8,128)S(1)} fusion(bf16[8,40,1024,1]{2,1,3,0:T(8,128)(2,1)S(1)} %bitcast.112, bf16[24,128,1024,1]{2,1,0,3:T(8,128)(2,1)S(1)} %bitcast.102), kind=kOutput, calls=%fused_computation.71 | convolution fusion | flops 2013265920 | bytes 10878976 | tf_op jit(solution)/shard_map/dot_general | solution.py:84
  87.2 0.5 pad_maximum_fusion
  87.7 2.7 %copy.46 = f32[8,41,24,128]{3,1,0,2:T(8,128)} copy(f32[8,41,24,128]{3,1,2,0:T(8,128)S(1)} %pad_maximum_fusion) | data formatting | bytes 8060928 | tf_op jit(solution)/shard_map/concatenate | solution.py:88
  90.4 3.1 %gather_fusion.1 = f32[8,41,16,128]{3,1,2,0:T(8,128)S(1)} fusion(f32[8,41,24,128]{3,1,0,2:T(8,128)} %copy.46, s32[8]{0:T(128)S(1)} %or_bitcast_fusion), kind=kCustom, calls=%fused_computation.1 | custom fusion | bytes 5374080 | tf_op jit(solution)/shard_map/vmap()/gather | solution.py:38
  93.5 2.4 %copy.47 = f32[8,41,16,128]{3,2,0,1:T(8,128)} copy(f32[8,41,16,128]{3,1,2,0:T(8,128)S(1)} %gather_fusion.1) | data formatting | bytes 5373952 | tf_op jit(solution)/shard_map/vmap()/gather | solution.py:38
  95.9 3.9 %reshape.51 = f32[8,41,2048]{2,0,1:T(8,128)} reshape(f32[8,41,16,128]{3,2,0,1:T(8,128)} %copy.47) | data formatting | bytes 5373952 | tf_op jit(solution)/shard_map/vmap()/reshape | solution.py:39
  99.8 0.1 convert_reduce_fusion.3
  100.2 0.7 copy-done.2
  100.9 0.3 convert_reduce_fusion.1
  101.4 5.5 %convert_reduce_fusion = (f32[3072]{0:T(1024)S(1)}, f32[3072]{0:T(1024)S(1)}) fusion(bf16[3072,1024]{1,0:T(8,128)(2,1)} %constant_dynamic-update-slice_fusion), kind=kLoop, calls=%fused_computation.7 | loop fusion | flops 12576768 | bytes 6316032 | tf_op jit(solution)/shard_map/reduce_sum | solution.py:102
  106.9 3.4 %all-reduce.1 = (f32[8,41]{1,0:T(8,128)S(1)}, f32[8,41]{1,0:T(8,128)S(1)}, f32[24,128]{1,0:T(8,128)S(1)}, f32[24,128]{1,0:T(8,128)S(1)}) all-reduce(f32[8,41]{1,0:T(8,128)S(1)} %get-tuple-element.50, f32[8,41]{1,0:T(8,128)S(1)} %get-tuple-element.49, ...), channel_id=1, replica_groups=mesh['parts'=2,'genes'=8,'samples'=2] {'samples'}, use_global_device_ids=true, to_apply=%region_12.13 | all-reduce | flops 6800 | bytes 54400 | tf_op jit(solution)/shard_map/psum | solution.py:104
  110.3 10.1 %while.3 = (s32[]{:T(128)}, f32[24,128]{1,0:T(8,128)S(1)}, s32[8,2]{0,1:T(2,128)S(1)}, f32[8,16,128]{2,1,0:T(8,128)S(1)}, s32[]{:T(128)}) while((s32[]{:T(128)}, f32[24,128]{1,0:T(8,128)S(1)}, s32[8,2]{0,1:T(2,128)S(1)}, f32[8,16,128]{2,1,0:T(8,128)S(1)}, s32[]{:T(128)}) %tuple.35), condition=%wide.while_cond.1, body=%wide.while_body.1.sunk | while | flops 2 | bytes 16481 | solution.py:38
  110.4 0.5 slice.35
  110.9 0.7 bitcast_dynamic-update-slice_fusion.5
  111.7 0.5 slice.35
  112.2 0.7 bitcast_dynamic-update-slice_fusion.5
  112.9 0.5 slice.35
  113.4 0.7 bitcast_dynamic-update-slice_fusion.5
  114.2 0.5 slice.35
  114.7 0.7 bitcast_dynamic-update-slice_fusion.5
  115.5 0.5 slice.35
  116.0 0.7 bitcast_dynamic-update-slice_fusion.5
  116.7 0.5 slice.35
  117.2 0.7 bitcast_dynamic-update-slice_fusion.5
  118.0 0.5 slice.35
  118.5 0.7 bitcast_dynamic-update-slice_fusion.5
  119.2 0.5 slice.35
  119.8 0.7 bitcast_dynamic-update-slice_fusion.5
  120.5 10.1 %while.2 = (s32[]{:T(128)}, f32[24,128]{1,0:T(8,128)S(1)}, s32[8,2]{0,1:T(2,128)S(1)}, f32[8,16,128]{2,1,0:T(8,128)S(1)}, s32[]{:T(128)}) while((s32[]{:T(128)}, f32[24,128]{1,0:T(8,128)S(1)}, s32[8,2]{0,1:T(2,128)S(1)}, f32[8,16,128]{2,1,0:T(8,128)S(1)}, s32[]{:T(128)}) %tuple.40), condition=%wide.while_cond, body=%wide.while_body.sunk | while | flops 2 | bytes 16481 | solution.py:38
  120.6 0.5 slice.34
  121.1 0.7 bitcast_dynamic-update-slice_fusion.4
  121.8 0.5 slice.34
  122.3 0.7 bitcast_dynamic-update-slice_fusion.4
  123.1 0.5 slice.34
  123.6 0.7 bitcast_dynamic-update-slice_fusion.4
  124.4 0.5 slice.34
  124.9 0.7 bitcast_dynamic-update-slice_fusion.4
  125.6 0.5 slice.34
  126.1 0.7 bitcast_dynamic-update-slice_fusion.4
  126.9 0.5 slice.34
  127.4 0.7 bitcast_dynamic-update-slice_fusion.4
  128.2 0.5 slice.34
  128.7 0.7 bitcast_dynamic-update-slice_fusion.4
  129.4 0.5 slice.34
  129.9 0.7 bitcast_dynamic-update-slice_fusion.4
  130.9 2.5 %multiply_convert_fusion = bf16[8,41,1024]{2,0,1:T(8,128)(2,1)} fusion(f32[8,41,1024]{2,0,1:T(8,128)} %reduce-scatter.2.cloned.1.call-done, f32[8,41]{0,1:T(8,128)S(1)} %copy.51, f32[8,1024]{1,0:T(8,128)S(1)} %get-tuple-element.48, f32[8,41]{0,1:T(8,128)S(1)} %copy.49, f32[8,1024]{1,0:T(8,128)S(1)} %get-tuple-element.47), kind=kLoop, calls=%fused_computation.16 | loop fusion | flops 2015232 | bytes 2083392 | tf_op jit(solution)/shard_map/convert_element_type | solution.py:57
  (63 shorter events, 2.5 us)
Async XLA Ops:
  6.5 4.5 %copy-start.7 = (s32[64]{0:T(128)S(1)}, s32[64]{0:T(128)}, u32[]{:S(2)}) copy-start(s32[64]{0:T(128)} %param.12) | copy-start | bytes 772
  6.5 4.5 %copy-start.3 = (bf16[128,2560]{1,0:T(8,128)(2,1)S(1)}, bf16[128,2560]{1,0:T(8,128)(2,1)}, u32[]{:S(2)}) copy-start(bf16[128,2560]{1,0:T(8,128)(2,1)} %param.9) | copy-start | bytes 1966084
  6.5 4.9 %copy-start.6 = (s32[64,8]{0,1:T(8,128)S(1)}, s32[64,8]{0,1:T(8,128)}, u32[]{:S(2)}) copy-start(s32[64,8]{0,1:T(8,128)} %param.10) | copy-start | bytes 6148
  6.5 5.0 %copy-start.5 = (s32[64,40]{0,1:T(8,128)S(1)}, s32[64,40]{0,1:T(8,128)}, u32[]{:S(2)}) copy-start(s32[64,40]{0,1:T(8,128)} %param.11) | copy-start | bytes 30724
  9.7 68.9 %collective-permute-start = (bf16[1024,1024]{1,0:T(8,128)(2,1)}, bf16[1024,1024]{1,0:T(8,128)(2,1)S(1)}, u32[]{:S(2)}, u32[]{:S(2)}) collective-permute-start(bf16[1024,1024]{1,0:T(8,128)(2,1)} %slice.3), channel_id=1, source_target_pairs={{2,0},{4,2},{6,4},{8,6},{10,8},{12,10},{14,12},{3,1},{5,3},{7,5},{... | collective-permute-start | bytes 6291464 | tf_op jit(solution)/shard_map/ppermute | solution.py:15
  12.4 16.1 %copy-start.8 = (s32[8]{0:T(128)S(1)}, s32[8]{0:T(128)}, u32[]{:S(2)}) copy-start(s32[8]{0:T(128)} %param.13) | copy-start | bytes 100
  19.9 58.6 %all-to-all-start = ((bf16[8,128,320]{1,2,0:T(8,128)(2,1)}), bf16[8,128,320]{1,2,0:T(8,128)(2,1)S(1)}, u32[]{:S(2)}, u32[]{:S(2)}) async-start(bf16[8,128,320]{1,2,0:T(8,128)(2,1)} %fusion.15), calls=%async_computation | async-start | bytes 1310720 | tf_op jit(solution)/shard_map/all_to_all | solution.py:74
  28.4 102.5 %reduce-scatter.2.cloned.1.call-start = ((), (), s32[]{:S(2)}) async-start(), calls=%async_computation.2 | async-start | bytes 4030464 | tf_op jit(solution)/shard_map/reduce_scatter | solution.py:108
  33.0 47.0 %copy-start.4 = (bf16[8,1024]{1,0:T(8,128)(2,1)S(1)}, bf16[8,1024]{1,0:T(8,128)(2,1)}, u32[]{:S(2)}) copy-start(bf16[8,1024]{1,0:T(8,128)(2,1)} %param.8) | copy-start | bytes 49156
  78.5 1.6 %copy-start.1 = (bf16[8,128,320]{1,2,0:T(8,128)(2,1)}, bf16[8,128,320]{1,2,0:T(8,128)(2,1)S(1)}, u32[]{:S(2)}) copy-start(bf16[8,128,320]{1,2,0:T(8,128)(2,1)S(1)} %all-to-all-done) | copy-start | bytes 1966084
  80.1 4.8 %copy-start = (bf16[3072,1024]{1,0:T(8,128)(2,1)S(1)}, bf16[3072,1024]{1,0:T(8,128)(2,1)}, u32[]{:S(2)}) copy-start(bf16[3072,1024]{1,0:T(8,128)(2,1)} %constant_dynamic-update-slice_fusion) | copy-start | bytes 18874372
  99.8 1.1 copy-start.2
Sparse Core Ops, SparseCore 0:
  99.9 7.5 reduce-scatter.1
